TPU v7x, 32 devices: a whole 2x2x4 slice. The times are simulated.
32 devices in a mesh: lat: 16 (over z, y, x), lon: 2 (over core).
Axes of the slice: x: 2, y: 2, z: 4, core: 2. Of those that a mesh axis runs over, the one named last changes fastest.
Arguments:
- fields: bfloat16 [2048, 2, 1024], P('lat', 'lon'), may hold values from -6 to 6
- proj_x: bfloat16 [1024, 1024], P('lon'), may hold values from -0.1875 to 0.1875
- proj_z: bfloat16 [1024, 1024], P('lon'), may hold values from -0.1875 to 0.1875
- proj_bc: bfloat16 [1024, 128], P('lon'), may hold values from -0.1875 to 0.1875
- proj_dt: bfloat16 [1024, 16], P('lon'), may hold values from -1 to 1
- conv_x: float32 [4, 1024], replicated, may hold values from -3 to 3
- conv_bc: float32 [4, 128], replicated, may hold values from -3 to 3
- dt_bias: float32 [16], replicated, may hold values from -1 to 0.5
- log_rate: float32 [16], replicated, may hold values from -12 to -2.7
- norm_gain: float32 [1024], replicated, may hold values from 0.1 to 1.9
- proj_out: bfloat16 [1024, 1024], P('lon'), may hold values from -0.1875 to 0.1875
Outputs:
- mixer_out: bfloat16 [2048, 2, 1024], P('lat', 'lon')
All inputs are finite; a program needn't handle non-finite values.
Results may differ from a plain program's by a relative error of at most 0.012.
Values may be sent and summed in bfloat16 or wider, within the bound.
A program may use at most 64 MiB of HBM per device.

v0:
```python
import jax
import jax.numpy as jnp
from jax import lax
from jax.sharding import PartitionSpec as P

norm_epsilon = 1e-05
highest = lax.Precision.HIGHEST


def shifted(block, axis, distance):
    devices = range(lax.axis_size(axis))
    route = [(i - distance, i) for i in devices if i - distance in devices]
    return lax.ppermute(block, axis, route)


def partner_2(block, axis, apart):
    count = lax.axis_size(axis)
    route = []
    for low in range(count):
        high = low | 1 << apart
        if high != low and high < count:
            route += [(low, high), (high, low)]
    return lax.ppermute(block, axis, route)


def causal_conv(values, kernel):
    out_rows = values.shape[0] - kernel.shape[0] + 1
    acc_sum = jnp.zeros((out_rows,) + values.shape[1:], jnp.float32)
    for offset in range(kernel.shape[0]):
        acc_sum = acc_sum + kernel[offset] * values[offset : offset + out_rows]
    return jax.nn.silu(acc_sum).astype(jnp.bfloat16)


def combine(earlier_part, later_part):
    return (
        earlier_part[0] + later_part[0],
        jnp.exp(later_part[0])[..., None] * earlier_part[1] + later_part[1],
    )


def local(
    fields,
    proj_x,
    proj_z,
    proj_bc,
    proj_dt,
    conv_x,
    conv_bc,
    dt_bias,
    log_rate,
    norm_gain,
    proj_out,
):
    band_rows, band_cols, model_width = fields.shape
    margin = conv_x.shape[0] - 1
    head_count = log_rate.shape[0]
    inner_width = proj_x.shape[1]
    state_size = proj_bc.shape[1] // 2
    row_count = fields.shape[0]
    flat_rows = fields.reshape(row_count * band_cols, model_width)
    pieces = (
        lax.all_gather(proj_x, "lon", axis=0, tiled=True),
        lax.all_gather(proj_z, "lon", axis=0, tiled=True),
        lax.all_gather(proj_bc, "lon", axis=0, tiled=True),
        lax.all_gather(proj_dt, "lon", axis=0, tiled=True),
    )
    columns = flat_rows
    projected = tuple(
        (jnp.dot(columns, piece_rows, preferred_element_type=jnp.float32) for piece_rows in pieces)
    )
    inner_pre, gate_pre, bc_pre, dt_pre = [
        result_sum.astype(jnp.bfloat16).reshape(row_count, band_cols, -1)
        for result_sum in projected
    ]
    tail_rows = shifted((inner_pre[band_rows - margin :], bc_pre[band_rows - margin :]), "lat", 1)
    inner_ext = jnp.concatenate([tail_rows[0], inner_pre], 0)
    bc_ext = jnp.concatenate([tail_rows[1], bc_pre], 0)
    inner_act = causal_conv(inner_ext.astype(jnp.float32), conv_x)
    bc_act = causal_conv(bc_ext.astype(jnp.float32), conv_bc)
    step_dt = jax.nn.softplus(dt_pre.astype(jnp.float32) + dt_bias)
    log_step = -jnp.exp(log_rate) * step_dt
    head_inner = inner_act.astype(jnp.float32).reshape(band_rows, band_cols, head_count, -1)
    input_b = bc_act[..., :state_size].astype(jnp.float32)
    read_c = bc_act[..., state_size:].astype(jnp.float32)
    cumulative = jnp.cumsum(log_step, axis=0)
    causal = jnp.arange(band_rows)[:, None] >= jnp.arange(band_rows)[None, :]
    decay_gap = cumulative[:, None] - cumulative[None, :]
    decay = jnp.exp(jnp.where(causal[:, :, None, None], decay_gap, -jnp.inf))
    scores = jnp.einsum("tcn,scn->tsc", read_c, input_b, precision=highest)
    weights = decay * scores[:, :, :, None] * step_dt[None]
    diag_out = jnp.einsum("tsch,schp->tchp", weights, head_inner, precision=highest)
    band_total = cumulative[-1]
    end_weight = jnp.exp(band_total[None] - cumulative) * step_dt
    end_state = jnp.einsum("sch,scn,schp->chnp", end_weight, input_b, head_inner, precision=highest)
    states = end_state.reshape(band_cols, head_count, -1)
    position = lax.axis_index("lat")
    prefix = (jnp.zeros_like(band_total), jnp.zeros_like(states))
    running = (band_total, states)
    for bit_level in range(lax.axis_size("lat").bit_length() - 1):
        partner = partner_2((running[0], running[1]), "lat", bit_level)
        later_half = position // (1 << bit_level) % 2 == 1
        merged_low = combine(partner, running)
        merged_high = combine(running, partner)
        moved_prefix = combine(partner, prefix)
        prefix = (
            jnp.where(later_half, moved_prefix[0], prefix[0]),
            jnp.where(later_half, moved_prefix[1], prefix[1]),
        )
        running = (
            jnp.where(later_half, merged_low[0], merged_high[0]),
            jnp.where(later_half, merged_low[1], merged_high[1]),
        )
    incoming = prefix[1]
    incoming = incoming.reshape(band_cols, head_count, state_size, -1)
    state_out = (
        jnp.einsum("tcn,chnp->tchp", read_c, incoming, precision=highest)
        * jnp.exp(cumulative)[..., None]
    )
    mixed_heads = (diag_out + state_out).reshape(band_rows, band_cols, inner_width)
    gated_out = mixed_heads * jax.nn.silu(gate_pre.astype(jnp.float32))
    normed = (
        gated_out
        * lax.rsqrt(jnp.mean(gated_out * gated_out, -1, keepdims=True) + norm_epsilon)
        * norm_gain
    )
    hidden = normed.astype(jnp.bfloat16).reshape(band_rows * band_cols, inner_width)
    columns = hidden
    result = jnp.dot(
        columns,
        lax.all_gather(proj_out, "lon", axis=0, tiled=True),
        preferred_element_type=jnp.float32,
    )
    return result.astype(jnp.bfloat16).reshape(band_rows, band_cols, model_width)


def solution(mesh):
    return jax.shard_map(
        local,
        mesh=mesh,
        in_specs=(
            P("lat", "lon", None),
            P("lon", None),
            P("lon", None),
            P("lon", None),
            P("lon", None),
            P(),
            P(),
            P(),
            P(),
            P(),
            P("lon", None),
        ),
        out_specs=P("lat", "lon", None),
        check_vma=False,
    )
```

profile of v0, /device:TPU:0, one launch (start us, length us, event | category | flops | bytes accessed | tf_op | source)
XLA Modules:
  0.0 81.1 jit_solution(3935069047673425926)
XLA Ops:
  6.5 0.7 all-gather.4.cloned.1.call-update
  7.3 2.2 %all_gather.16 = bf16[1024,16]{0,1:T(8,128)(2,1)S(1)} all-gather(bf16[512,16]{0,1:T(8,128)(2,1)} %param.15), channel_id=1, replica_groups=mesh['lat'=16,'lon'=2] {'lon'}, dimensions={0}, use_global_device_ids=true | all-gather | bytes 49152 | tf_op jit(solution)/shard_map/all_gather | solution.py:65
  9.5 0.7 exponential_negate_fusion
  10.2 0.9 %compare_select_fusion = f32[128,16]{0,1:T(8,128)S(1)} fusion(bf16[1024,16]{0,1:T(8,128)(2,1)S(1)} %all_gather.16, bf16[128,1,1024]{2,0,1:T(8,128)(2,1)S(1)} %copy-done, f32[16]{0:T(128)} %param.18), kind=kOutput, calls=%fused_computation.69 | convolution fusion | flops 4212736 | bytes 303168 | tf_op jit(solution)/shard_map/dot_general | solution.py:69
  11.3 2.9 %collective-permute-start.2 = (f32[1,16]{1,0:T(1,128)S(1)}, f32[1,16]{1,0:T(1,128)S(1)}, u32[]{:S(2)}, u32[]{:S(2)}) collective-permute-start(f32[1,16]{1,0:T(1,128)S(1)} %get-tuple-element.11), channel_id=1, source_target_pairs={{0,2},{2,0},{4,6},{6,4},{8,10},{10,8},{12,14},{14,12},{16,18},{18,... | collective-permute-start | bytes 200 | tf_op jit(solution)/shard_map/ppermute | solution.py:23
  14.2 2.2 %all_gather.17 = bf16[1024,128]{1,0:T(8,128)(2,1)S(1)} all-gather(bf16[512,128]{1,0:T(8,128)(2,1)} %param.14), channel_id=1, replica_groups=mesh['lat'=16,'lon'=2] {'lon'}, dimensions={0}, use_global_device_ids=true | all-gather | bytes 393216 | tf_op jit(solution)/shard_map/all_gather | solution.py:64
  16.4 0.2 convolution_convert_fusion.3
  16.7 1.9 %collective-permute-start.1 = (bf16[3,1,128]{2,0,1:T(4,128)(2,1)S(1)}, bf16[3,1,128]{2,0,1:T(4,128)(2,1)S(1)}, u32[]{:S(2)}, u32[]{:S(2)}) collective-permute-start(bf16[3,1,128]{2,0,1:T(4,128)(2,1)S(1)} %slice_bitcast_fusion.3), channel_id=1, source_target_pairs={{0,2},{2,4},{4,6},{6,8},{8,10},{10,12},{12,14},{14,16},{16,18},{18... | collective-permute-start | bytes 2312 | tf_op jit(solution)/shard_map/ppermute | solution.py:13
  18.9 2.1 %collective-permute-start.3 = (f32[1,16]{1,0:T(1,128)S(1)}, f32[1,16]{1,0:T(1,128)S(1)}, u32[]{:S(2)}, u32[]{:S(2)}) collective-permute-start(f32[1,16]{1,0:T(1,128)S(1)} %get-tuple-element.10), channel_id=1, source_target_pairs={{0,4},{4,0},{2,6},{6,2},{8,12},{12,8},{10,14},{14,10},{16,20},{20,... | collective-permute-start | bytes 200 | tf_op jit(solution)/shard_map/ppermute | solution.py:23
  21.1 1.1 %all-gather.4.cloned.1.call-done = bf16[1024,1024]{1,0:T(8,128)(2,1)} async-done(((bf16[512,1024]{1,0:T(8,128)(2,1)}), bf16[1024,1024]{1,0:T(8,128)(2,1)}) %all-gather.4.cloned.1.call-update) | async-done | bytes 2097168 | tf_op jit(solution)/shard_map/all_gather | solution.py:62
  22.2 2.0 %convolution_convert_fusion.2 = bf16[128,1024]{1,0:T(8,128)(2,1)S(1)} fusion(bf16[1024,1024]{1,0:T(8,128)(2,1)} %all-gather.4.cloned.1.call-done, bf16[128,1,1024]{2,0,1:T(8,128)(2,1)S(1)} %copy-done), kind=kOutput, calls=%fused_computation.7 | convolution fusion | flops 268566528 | bytes 2621440 | tf_op jit(solution)/shard_map/dot_general | solution.py:69
  24.3 3.6 %collective-permute-start = (bf16[3,1,1024]{2,0,1:T(4,128)(2,1)S(1)}, bf16[3,1,1024]{2,0,1:T(4,128)(2,1)S(1)}, u32[]{:S(2)}, u32[]{:S(2)}) collective-permute-start(bf16[3,1,1024]{2,0,1:T(4,128)(2,1)S(1)} %slice_bitcast_fusion.2), channel_id=1, source_target_pairs={{0,2},{2,4},{4,6},{6,8},{8,10},{10,12},{12,14},{14,16},{16,18},{18... | collective-permute-start | bytes 18440 | tf_op jit(solution)/shard_map/ppermute | solution.py:13
  28.0 1.3 %collective-permute-done = bf16[3,1,1024]{2,0,1:T(4,128)(2,1)S(1)} collective-permute-done((bf16[3,1,1024]{2,0,1:T(4,128)(2,1)S(1)}, bf16[3,1,1024]{2,0,1:T(4,128)(2,1)S(1)}, u32[]{:S(2)}, u32[]{:S(2)}) %collective-permute-start) | collective-permute-done | bytes 6176 | tf_op jit(solution)/shard_map/ppermute | solution.py:13
  29.3 0.3 multiply_convert_fusion.1
  29.9 0.5 fusion.14
  30.6 2.3 %collective-permute-start.5 = (f32[1,16,4096]{2,1,0:T(8,128)S(1)}, f32[1,16,4096]{2,1,0:T(8,128)S(1)}, u32[]{:S(2)}, u32[]{:S(2)}) collective-permute-start(f32[1,16,4096]{2,1,0:T(8,128)S(1)} %reshape.305), channel_id=1, source_target_pairs={{0,2},{2,0},{4,6},{6,4},{8,10},{10,8},{12,14},{14,12},{16,18},{18,... | collective-permute-start | bytes 786440 | tf_op jit(solution)/shard_map/ppermute | solution.py:23
  32.9 3.6 %collective-permute-start.4 = (f32[1,16]{1,0:T(1,128)S(1)}, f32[1,16]{1,0:T(1,128)S(1)}, u32[]{:S(2)}, u32[]{:S(2)}) collective-permute-start(f32[1,16]{1,0:T(1,128)S(1)} %get-tuple-element.8), channel_id=1, source_target_pairs={{0,8},{8,0},{2,10},{10,2},{4,12},{12,4},{6,14},{14,6},{16,24},{24,... | collective-permute-start | bytes 200 | tf_op jit(solution)/shard_map/ppermute | solution.py:23
  36.5 1.5 %collective-permute-done.4 = f32[1,16]{1,0:T(1,128)S(1)} collective-permute-done((f32[1,16]{1,0:T(1,128)S(1)}, f32[1,16]{1,0:T(1,128)S(1)}, u32[]{:S(2)}, u32[]{:S(2)}) %collective-permute-start.4) | collective-permute-done | bytes 96 | tf_op jit(solution)/shard_map/ppermute | solution.py:23
  38.1 0.5 collective-permute-done.5
  38.7 2.7 %collective-permute-start.6 = (f32[1,16,4096]{2,1,0:T(8,128)S(1)}, f32[1,16,4096]{2,1,0:T(8,128)S(1)}, u32[]{:S(2)}, u32[]{:S(2)}) collective-permute-start(f32[1,16,4096]{2,1,0:T(8,128)S(1)} %add_select_fusion.5), channel_id=1, source_target_pairs={{0,4},{4,0},{2,6},{6,2},{8,12},{12,8},{10,14},{14,10},{16,20},{20,... | collective-permute-start | bytes 786440 | tf_op jit(solution)/shard_map/ppermute | solution.py:23
  41.4 4.4 %collective-permute-done.6 = f32[1,16,4096]{2,1,0:T(8,128)S(1)} collective-permute-done((f32[1,16,4096]{2,1,0:T(8,128)S(1)}, f32[1,16,4096]{2,1,0:T(8,128)S(1)}, u32[]{:S(2)}, u32[]{:S(2)}) %collective-permute-start.6) | collective-permute-done | bytes 262176 | tf_op jit(solution)/shard_map/ppermute | solution.py:23
  45.9 3.7 %collective-permute-start.7 = (f32[1,16,4096]{2,1,0:T(8,128)S(1)}, f32[1,16,4096]{2,1,0:T(8,128)S(1)}, u32[]{:S(2)}, u32[]{:S(2)}) collective-permute-start(f32[1,16,4096]{2,1,0:T(8,128)S(1)} %add_select_fusion.4), channel_id=1, source_target_pairs={{0,8},{8,0},{2,10},{10,2},{4,12},{12,4},{6,14},{14,6},{16,24},{24,... | collective-permute-start | bytes 786440 | tf_op jit(solution)/shard_map/ppermute | solution.py:23
  49.6 6.6 %collective-permute-done.7 = f32[1,16,4096]{2,1,0:T(8,128)S(1)} collective-permute-done((f32[1,16,4096]{2,1,0:T(8,128)S(1)}, f32[1,16,4096]{2,1,0:T(8,128)S(1)}, u32[]{:S(2)}, u32[]{:S(2)}) %collective-permute-start.7) | collective-permute-done | bytes 262176 | tf_op jit(solution)/shard_map/ppermute | solution.py:23
  56.4 3.4 %collective-permute-start.8 = (f32[1,16,4096]{2,1,0:T(8,128)S(1)}, f32[1,16,4096]{2,1,0:T(8,128)S(1)}, u32[]{:S(2)}, u32[]{:S(2)}) collective-permute-start(f32[1,16,4096]{2,1,0:T(8,128)S(1)} %add_select_fusion.3), channel_id=1, source_target_pairs={{0,16},{16,0},{2,18},{18,2},{4,20},{20,4},{6,22},{22,6},{8,24},{24... | collective-permute-start | bytes 786440 | tf_op jit(solution)/shard_map/ppermute | solution.py:23
  59.8 0.2 convolution_bitcast_fusion.2
  60.1 6.8 %collective-permute-done.8 = f32[1,16,4096]{2,1,0:T(8,128)S(1)} collective-permute-done((f32[1,16,4096]{2,1,0:T(8,128)S(1)}, f32[1,16,4096]{2,1,0:T(8,128)S(1)}, u32[]{:S(2)}, u32[]{:S(2)}) %collective-permute-start.8) | collective-permute-done | bytes 262176 | tf_op jit(solution)/shard_map/ppermute | solution.py:23
  67.1 0.2 reshape.306
  67.3 0.6 fusion.1
  68.0 1.3 %fusion = f32[128,1,16,64]{0,3,2,1:T(8,128)S(1)} fusion(f32[128,1,16,64]{0,3,2,1:T(8,128)S(1)} %fusion.1, bf16[128,16,64]{0,2,1:T(8,128)(2,1)S(1)} %bitcast.106, f32[128,16]{0,1:T(8,128)S(1)} %compare_select_fusion, f32[128,128]{1,0:T(8,128)S(1)} %copy.23, f32[128,16]{0,1:T(8,128)S(1)} %bitcast.109, pred[128,128]{1,0:T(8,128)(4,1)S(1)} %iota_compare_fusion), kind=kOutput, calls=%fused_computation.2 | convolution fusion | flops 202506240 | bytes 1409024 | tf_op jit(solution)/shard_map/tsch,schp->tchp/dot_general | solution.py:91
  69.3 0.2 copy.27
  69.5 2.2 %multiply_reduce_fusion = (f32[128]{0:T(128)S(1)}, f32[128,1024]{1,0:T(8,128)S(1)}) fusion(f32[128,1024]{1,0:T(8,128)S(1)} %copy.27, bf16[1024,1024]{1,0:T(8,128)(2,1)} %all-gather.6.cloned.1.call-done, bf16[128,1,1024]{2,0,1:T(8,128)(2,1)S(1)} %copy-done), kind=kOutput, calls=%fused_computation.27 | convolution fusion | flops 269614976 | bytes 3408384 | tf_op jit(solution)/shard_map/dot_general | solution.py:69
  71.7 2.8 %fusion.3 = bf16[128,1,1024]{2,0,1:T(8,128)(2,1)} fusion(bf16[1024,1024]{1,0:T(8,128)(2,1)} %all-gather.8.cloned.1.call-done, f32[128,1024]{1,0:T(8,128)S(1)} %get-tuple-element.28, f32[1024]{0:T(1024)S(1)} %copy-done.2, f32[128]{0:T(128)S(1)} %add_rsqrt_fusion), kind=kOutput, calls=%fused_computation.8 | convolution fusion | flops 268959744 | bytes 2888192 | tf_op jit(solution)/shard_map/dot_general | solution.py:128
  (47 shorter events, 1.9 us)
Async XLA Ops:
  6.5 3.6 %copy-start = (bf16[128,1,1024]{2,0,1:T(8,128)(2,1)S(1)}, bf16[128,1,1024]{2,0,1:T(8,128)(2,1)}, u32[]{:S(2)}) copy-start(bf16[128,1,1024]{2,0,1:T(8,128)(2,1)} %param.11) | copy-start | bytes 786436
  6.5 12.2 %copy-start.3 = (f32[4,128]{1,0:T(4,128)S(1)}, f32[4,128]{1,0:T(4,128)}, u32[]{:S(2)}) copy-start(f32[4,128]{1,0:T(4,128)} %param.17) | copy-start | bytes 6148
  6.5 12.3 %copy-start.1 = (f32[4,1024]{1,0:T(4,128)S(1)}, f32[4,1024]{1,0:T(4,128)}, u32[]{:S(2)}) copy-start(f32[4,1024]{1,0:T(4,128)} %param.16) | copy-start | bytes 49156
  6.5 15.7 %all-gather.4.cloned.1.call-start = ((), (), s32[]{:S(2)}) async-start(), calls=%async_computation | async-start | bytes 3145728 | tf_op jit(solution)/shard_map/all_gather | solution.py:62
  7.3 62.2 %all-gather.6.cloned.1.call-start = ((), (), s32[]{:S(2)}) async-start(), calls=%async_computation.1 | async-start | bytes 3145728 | tf_op jit(solution)/shard_map/all_gather | solution.py:63
  11.3 7.6 %collective-permute-start.2 = (f32[1,16]{1,0:T(1,128)S(1)}, f32[1,16]{1,0:T(1,128)S(1)}, u32[]{:S(2)}, u32[]{:S(2)}) collective-permute-start(f32[1,16]{1,0:T(1,128)S(1)} %get-tuple-element.11), channel_id=1, source_target_pairs={{0,2},{2,0},{4,6},{6,4},{8,10},{10,8},{12,14},{14,12},{16,18},{18,... | collective-permute-start | bytes 200 | tf_op jit(solution)/shard_map/ppermute | solution.py:23
  16.7 4.4 %collective-permute-start.1 = (bf16[3,1,128]{2,0,1:T(4,128)(2,1)S(1)}, bf16[3,1,128]{2,0,1:T(4,128)(2,1)S(1)}, u32[]{:S(2)}, u32[]{:S(2)}) collective-permute-start(bf16[3,1,128]{2,0,1:T(4,128)(2,1)S(1)} %slice_bitcast_fusion.3), channel_id=1, source_target_pairs={{0,2},{2,4},{4,6},{6,8},{8,10},{10,12},{12,14},{14,16},{16,18},{18... | collective-permute-start | bytes 2312 | tf_op jit(solution)/shard_map/ppermute | solution.py:13
  18.6 53.1 %all-gather.8.cloned.1.call-start = ((), (), s32[]{:S(2)}) async-start(), calls=%async_computation.2 | async-start | bytes 3145728 | tf_op jit(solution)/shard_map/all_gather | solution.py:130
  18.9 14.0 %collective-permute-start.3 = (f32[1,16]{1,0:T(1,128)S(1)}, f32[1,16]{1,0:T(1,128)S(1)}, u32[]{:S(2)}, u32[]{:S(2)}) collective-permute-start(f32[1,16]{1,0:T(1,128)S(1)} %get-tuple-element.10), channel_id=1, source_target_pairs={{0,4},{4,0},{2,6},{6,2},{8,12},{12,8},{10,14},{14,10},{16,20},{20,... | collective-permute-start | bytes 200 | tf_op jit(solution)/shard_map/ppermute | solution.py:23
  24.3 5.0 %collective-permute-start = (bf16[3,1,1024]{2,0,1:T(4,128)(2,1)S(1)}, bf16[3,1,1024]{2,0,1:T(4,128)(2,1)S(1)}, u32[]{:S(2)}, u32[]{:S(2)}) collective-permute-start(bf16[3,1,1024]{2,0,1:T(4,128)(2,1)S(1)} %slice_bitcast_fusion.2), channel_id=1, source_target_pairs={{0,2},{2,4},{4,6},{6,8},{8,10},{10,12},{12,14},{14,16},{16,18},{18... | collective-permute-start | bytes 18440 | tf_op jit(solution)/shard_map/ppermute | solution.py:13
  30.6 8.0 %collective-permute-start.5 = (f32[1,16,4096]{2,1,0:T(8,128)S(1)}, f32[1,16,4096]{2,1,0:T(8,128)S(1)}, u32[]{:S(2)}, u32[]{:S(2)}) collective-permute-start(f32[1,16,4096]{2,1,0:T(8,128)S(1)} %reshape.305), channel_id=1, source_target_pairs={{0,2},{2,0},{4,6},{6,4},{8,10},{10,8},{12,14},{14,12},{16,18},{18,... | collective-permute-start | bytes 786440 | tf_op jit(solution)/shard_map/ppermute | solution.py:23
  32.9 5.1 %collective-permute-start.4 = (f32[1,16]{1,0:T(1,128)S(1)}, f32[1,16]{1,0:T(1,128)S(1)}, u32[]{:S(2)}, u32[]{:S(2)}) collective-permute-start(f32[1,16]{1,0:T(1,128)S(1)} %get-tuple-element.8), channel_id=1, source_target_pairs={{0,8},{8,0},{2,10},{10,2},{4,12},{12,4},{6,14},{14,6},{16,24},{24,... | collective-permute-start | bytes 200 | tf_op jit(solution)/shard_map/ppermute | solution.py:23
  38.7 7.1 %collective-permute-start.6 = (f32[1,16,4096]{2,1,0:T(8,128)S(1)}, f32[1,16,4096]{2,1,0:T(8,128)S(1)}, u32[]{:S(2)}, u32[]{:S(2)}) collective-permute-start(f32[1,16,4096]{2,1,0:T(8,128)S(1)} %add_select_fusion.5), channel_id=1, source_target_pairs={{0,4},{4,0},{2,6},{6,2},{8,12},{12,8},{10,14},{14,10},{16,20},{20,... | collective-permute-start | bytes 786440 | tf_op jit(solution)/shard_map/ppermute | solution.py:23
  45.9 10.4 %collective-permute-start.7 = (f32[1,16,4096]{2,1,0:T(8,128)S(1)}, f32[1,16,4096]{2,1,0:T(8,128)S(1)}, u32[]{:S(2)}, u32[]{:S(2)}) collective-permute-start(f32[1,16,4096]{2,1,0:T(8,128)S(1)} %add_select_fusion.4), channel_id=1, source_target_pairs={{0,8},{8,0},{2,10},{10,2},{4,12},{12,4},{6,14},{14,6},{16,24},{24,... | collective-permute-start | bytes 786440 | tf_op jit(solution)/shard_map/ppermute | solution.py:23
  56.4 10.6 %collective-permute-start.8 = (f32[1,16,4096]{2,1,0:T(8,128)S(1)}, f32[1,16,4096]{2,1,0:T(8,128)S(1)}, u32[]{:S(2)}, u32[]{:S(2)}) collective-permute-start(f32[1,16,4096]{2,1,0:T(8,128)S(1)} %add_select_fusion.3), channel_id=1, source_target_pairs={{0,16},{16,0},{2,18},{18,2},{4,20},{20,4},{6,22},{22,6},{8,24},{24... | collective-permute-start | bytes 786440 | tf_op jit(solution)/shard_map/ppermute | solution.py:23
  69.5 2.3 %copy-start.2 = (f32[1024]{0:T(1024)S(1)}, f32[1024]{0:T(1024)}, u32[]{:S(2)}) copy-start(f32[1024]{0:T(1024)} %param.20) | copy-start | bytes 12292
Sparse Core Ops, SparseCore 0:
  8.9 13.2 all-gather.3
  23.8 11.7 all-gather.5
  49.7 8.9 all-gather.7
where the time goes:
time: 81.4 us; the launch traced here: 81.1 us
  starting transfers between devices  26.3 us (32%)
  waiting for transfers between devices  23 us (28%)
  between operations  13.4 us (16%)
  matrix products  10.8 us (13%)
  blocking collectives  4.38 us (5%)
  other arithmetic  1.99 us (2%)
  local copies, waits for them, and re-layouts  1.17 us (1%)
    ppermute x7, starting transfers between devices, partner_2(): return lax.ppermute(block, axis, route)  20.7 us
    ppermute x7, waiting for transfers between devices, partner_2(): return lax.ppermute(block, axis, route)  19.9 us
    ppermute x2, starting transfers between devices, shifted(): return lax.ppermute(block, axis, route)  5.56 us
    dot_general x4, matrix products, local(): jnp.dot(columns, piece_rows, preferred_element_type=jnp.float32)  5.28 us
    dot_general x1, matrix products, local(): jnp.dot(columns, lax.all_gather(proj_out, 'lon', axis=0, tiled=True), pre...  2.81 us
    all_gather x1, blocking collectives, local(): lax.all_gather(proj_bc, 'lon', axis=0, tiled=True)  2.19 us
    all_gather x1, blocking collectives, local(): lax.all_gather(proj_dt, 'lon', axis=0, tiled=True)  2.19 us
  transfers between devices with their start and end apart: 12, of which 7 were waited for; matrix products, arithmetic and copies ran while one was open for 14% of the time, Pallas kernels for 0%

commit v1 on v0

--- a/solution.py
+++ b/solution.py
@@ -62,7 +62,12 @@
         lax.all_gather(proj_x, "lon", axis=0, tiled=True),
         lax.all_gather(proj_z, "lon", axis=0, tiled=True),
         lax.all_gather(proj_bc, "lon", axis=0, tiled=True),
-        lax.all_gather(proj_dt, "lon", axis=0, tiled=True),
+        jnp.concatenate(
+            jax.lax.all_to_all(
+                jnp.stack([proj_dt for _ in range(jax.lax.axis_size("lon"))], axis=0), "lon", 0, 0
+            ),
+            axis=0,
+        ),
     )
     columns = flat_rows
     projected = tuple(

time: 81.4 us -> 83.9 us (1.031)
  starting transfers between devices: 26.3 us -> 28 us
  blocking collectives: 4.38 us -> 5.93 us
  waiting for transfers between devices: 23 us -> 21.5 us
    all_to_all x0 -> x1, blocking collectives: none -> 3.73 us  [local(): jax.lax.all_to_all(jnp.stack([proj_dt for _ in range(jax.lax.axis_size('l...]
    all_gather x1 -> x0, blocking collectives: 2.19 us -> none  [local(): lax.all_gather(proj_dt, 'lon', axis=0, tiled=True)]
    all_gather x1, waiting for transfers between devices: 1.1 us -> 0.02 us  [local(): lax.all_gather(proj_x, 'lon', axis=0, tiled=True)]
    ppermute x7, starting transfers between devices: 20.7 us -> 21.6 us  [partner_2(): return lax.ppermute(block, axis, route)]
  transfers between devices with their start and end apart: 12 -> 12, of which waited for: 7 -> 5; matrix products, arithmetic and copies ran while one was open for 14% -> 14% of each run, Pallas kernels for 0% -> 0%
where the time goes in v1:
time: 83.9 us; the launch traced here: 83.6 us
  starting transfers between devices  28 us (33%)
  waiting for transfers between devices  21.5 us (26%)
  between operations  13.5 us (16%)
  matrix products  10.8 us (13%)
  blocking collectives  5.93 us (7%)
  other arithmetic  2.79 us (3%)
  local copies, waits for them, and re-layouts  1.17 us (1%)
    ppermute x7, starting transfers between devices, partner_2(): return lax.ppermute(block, axis, route)  21.6 us
    ppermute x7, waiting for transfers between devices, partner_2(): return lax.ppermute(block, axis, route)  19.4 us
    ppermute x2, starting transfers between devices, shifted(): return lax.ppermute(block, axis, route)  6.28 us
    dot_general x4, matrix products, local(): jnp.dot(columns, piece_rows, preferred_element_type=jnp.float32)  5.29 us
    all_to_all x1, blocking collectives, local(): jax.lax.all_to_all(jnp.stack([proj_dt for _ in range(jax.lax.axis_size('l...  3.73 us
    dot_general x1, matrix products, local(): jnp.dot(columns, lax.all_gather(proj_out, 'lon', axis=0, tiled=True), pre...  2.81 us
    all_gather x1, blocking collectives, local(): lax.all_gather(proj_bc, 'lon', axis=0, tiled=True)  2.19 us
  transfers between devices with their start and end apart: 12, of which 5 were waited for; matrix products, arithmetic and copies ran while one was open for 14% of the time, Pallas kernels for 0%

profile of v1, /device:TPU:0, one launch (start us, length us, event | category | flops | bytes accessed | tf_op | source)
XLA Modules:
  0.0 83.6 jit_solution(12960277766635121128)
XLA Ops:
  6.5 0.7 all-gather.4.cloned.1.call-update
  7.3 0.8 pad_maximum_fusion
  8.1 3.7 %all_to_all.5 = bf16[2,512,16]{1,2,0:T(8,128)(2,1)S(1)} all-to-all(bf16[2,512,16]{1,2,0:T(8,128)(2,1)S(1)} %pad_maximum_fusion), channel_id=1, replica_groups=mesh['lat'=16,'lon'=2] {'lon'}, dimensions={0} | all-to-all | bytes 65536 | tf_op jit(solution)/shard_map/all_to_all | solution.py:66
  11.8 0.7 exponential_negate_fusion
  12.5 0.9 %compare_select_fusion = f32[128,16]{0,1:T(8,128)S(1)} fusion(bf16[1024,16]{0,1:T(8,128)(2,1)S(1)} %bitcast.117, bf16[128,1,1024]{2,0,1:T(8,128)(2,1)S(1)} %copy-done, f32[16]{0:T(128)} %param.18), kind=kOutput, calls=%fused_computation.71 | convolution fusion | flops 4212736 | bytes 303168 | tf_op jit(solution)/shard_map/dot_general | solution.py:74
  13.7 3.0 %collective-permute-start.2 = (f32[1,16]{1,0:T(1,128)S(1)}, f32[1,16]{1,0:T(1,128)S(1)}, u32[]{:S(2)}, u32[]{:S(2)}) collective-permute-start(f32[1,16]{1,0:T(1,128)S(1)} %get-tuple-element.11), channel_id=1, source_target_pairs={{0,2},{2,0},{4,6},{6,4},{8,10},{10,8},{12,14},{14,12},{16,18},{18,... | collective-permute-start | bytes 200 | tf_op jit(solution)/shard_map/ppermute | solution.py:23
  16.7 2.2 %all_gather.13 = bf16[1024,128]{1,0:T(8,128)(2,1)S(1)} all-gather(bf16[512,128]{1,0:T(8,128)(2,1)} %param.14), channel_id=1, replica_groups=mesh['lat'=16,'lon'=2] {'lon'}, dimensions={0}, use_global_device_ids=true | all-gather | bytes 393216 | tf_op jit(solution)/shard_map/all_gather | solution.py:64
  18.9 0.2 convolution_convert_fusion.3
  19.2 1.9 %collective-permute-start.1 = (bf16[3,1,128]{2,0,1:T(4,128)(2,1)S(1)}, bf16[3,1,128]{2,0,1:T(4,128)(2,1)S(1)}, u32[]{:S(2)}, u32[]{:S(2)}) collective-permute-start(bf16[3,1,128]{2,0,1:T(4,128)(2,1)S(1)} %slice_bitcast_fusion.3), channel_id=1, source_target_pairs={{0,2},{2,4},{4,6},{6,8},{8,10},{10,12},{12,14},{14,16},{16,18},{18... | collective-permute-start | bytes 2312 | tf_op jit(solution)/shard_map/ppermute | solution.py:13
  21.4 2.1 %collective-permute-start.3 = (f32[1,16]{1,0:T(1,128)S(1)}, f32[1,16]{1,0:T(1,128)S(1)}, u32[]{:S(2)}, u32[]{:S(2)}) collective-permute-start(f32[1,16]{1,0:T(1,128)S(1)} %get-tuple-element.10), channel_id=1, source_target_pairs={{0,4},{4,0},{2,6},{6,2},{8,12},{12,8},{10,14},{14,10},{16,20},{20,... | collective-permute-start | bytes 200 | tf_op jit(solution)/shard_map/ppermute | solution.py:23
  23.6 2.0 %convolution_convert_fusion.2 = bf16[128,1024]{1,0:T(8,128)(2,1)S(1)} fusion(bf16[1024,1024]{1,0:T(8,128)(2,1)} %all-gather.4.cloned.1.call-done, bf16[128,1,1024]{2,0,1:T(8,128)(2,1)S(1)} %copy-done), kind=kOutput, calls=%fused_computation.7 | convolution fusion | flops 268566528 | bytes 2621440 | tf_op jit(solution)/shard_map/dot_general | solution.py:74
  25.7 4.3 %collective-permute-start = (bf16[3,1,1024]{2,0,1:T(4,128)(2,1)S(1)}, bf16[3,1,1024]{2,0,1:T(4,128)(2,1)S(1)}, u32[]{:S(2)}, u32[]{:S(2)}) collective-permute-start(bf16[3,1,1024]{2,0,1:T(4,128)(2,1)S(1)} %slice_bitcast_fusion.2), channel_id=1, source_target_pairs={{0,2},{2,4},{4,6},{6,8},{8,10},{10,12},{12,14},{14,16},{16,18},{18... | collective-permute-start | bytes 18440 | tf_op jit(solution)/shard_map/ppermute | solution.py:13
  30.1 1.3 %collective-permute-done = bf16[3,1,1024]{2,0,1:T(4,128)(2,1)S(1)} collective-permute-done((bf16[3,1,1024]{2,0,1:T(4,128)(2,1)S(1)}, bf16[3,1,1024]{2,0,1:T(4,128)(2,1)S(1)}, u32[]{:S(2)}, u32[]{:S(2)}) %collective-permute-start) | collective-permute-done | bytes 6176 | tf_op jit(solution)/shard_map/ppermute | solution.py:13
  31.5 0.3 multiply_convert_fusion.1
  32.0 0.5 fusion.15
  32.5 0.2 reshape.309
  32.7 2.6 %collective-permute-start.5 = (f32[1,16,4096]{2,1,0:T(8,128)S(1)}, f32[1,16,4096]{2,1,0:T(8,128)S(1)}, u32[]{:S(2)}, u32[]{:S(2)}) collective-permute-start(f32[1,16,4096]{2,1,0:T(8,128)S(1)} %reshape.309), channel_id=1, source_target_pairs={{0,2},{2,0},{4,6},{6,4},{8,10},{10,8},{12,14},{14,12},{16,18},{18,... | collective-permute-start | bytes 786440 | tf_op jit(solution)/shard_map/ppermute | solution.py:23
  35.3 3.7 %collective-permute-start.4 = (f32[1,16]{1,0:T(1,128)S(1)}, f32[1,16]{1,0:T(1,128)S(1)}, u32[]{:S(2)}, u32[]{:S(2)}) collective-permute-start(f32[1,16]{1,0:T(1,128)S(1)} %get-tuple-element.8), channel_id=1, source_target_pairs={{0,8},{8,0},{2,10},{10,2},{4,12},{12,4},{6,14},{14,6},{16,24},{24,... | collective-permute-start | bytes 200 | tf_op jit(solution)/shard_map/ppermute | solution.py:23
  39.0 1.5 %collective-permute-done.4 = f32[1,16]{1,0:T(1,128)S(1)} collective-permute-done((f32[1,16]{1,0:T(1,128)S(1)}, f32[1,16]{1,0:T(1,128)S(1)}, u32[]{:S(2)}, u32[]{:S(2)}) %collective-permute-start.4) | collective-permute-done | bytes 96 | tf_op jit(solution)/shard_map/ppermute | solution.py:23
  40.7 2.9 %collective-permute-start.6 = (f32[1,16,4096]{2,1,0:T(8,128)S(1)}, f32[1,16,4096]{2,1,0:T(8,128)S(1)}, u32[]{:S(2)}, u32[]{:S(2)}) collective-permute-start(f32[1,16,4096]{2,1,0:T(8,128)S(1)} %add_select_fusion.5), channel_id=1, source_target_pairs={{0,4},{4,0},{2,6},{6,2},{8,12},{12,8},{10,14},{14,10},{16,20},{20,... | collective-permute-start | bytes 786440 | tf_op jit(solution)/shard_map/ppermute | solution.py:23
  43.6 4.4 %collective-permute-done.6 = f32[1,16,4096]{2,1,0:T(8,128)S(1)} collective-permute-done((f32[1,16,4096]{2,1,0:T(8,128)S(1)}, f32[1,16,4096]{2,1,0:T(8,128)S(1)}, u32[]{:S(2)}, u32[]{:S(2)}) %collective-permute-start.6) | collective-permute-done | bytes 262176 | tf_op jit(solution)/shard_map/ppermute | solution.py:23
  48.1 3.9 %collective-permute-start.7 = (f32[1,16,4096]{2,1,0:T(8,128)S(1)}, f32[1,16,4096]{2,1,0:T(8,128)S(1)}, u32[]{:S(2)}, u32[]{:S(2)}) collective-permute-start(f32[1,16,4096]{2,1,0:T(8,128)S(1)} %add_select_fusion.4), channel_id=1, source_target_pairs={{0,8},{8,0},{2,10},{10,2},{4,12},{12,4},{6,14},{14,6},{16,24},{24,... | collective-permute-start | bytes 786440 | tf_op jit(solution)/shard_map/ppermute | solution.py:23
  52.1 6.6 %collective-permute-done.7 = f32[1,16,4096]{2,1,0:T(8,128)S(1)} collective-permute-done((f32[1,16,4096]{2,1,0:T(8,128)S(1)}, f32[1,16,4096]{2,1,0:T(8,128)S(1)}, u32[]{:S(2)}, u32[]{:S(2)}) %collective-permute-start.7) | collective-permute-done | bytes 262176 | tf_op jit(solution)/shard_map/ppermute | solution.py:23
  58.9 3.4 %collective-permute-start.8 = (f32[1,16,4096]{2,1,0:T(8,128)S(1)}, f32[1,16,4096]{2,1,0:T(8,128)S(1)}, u32[]{:S(2)}, u32[]{:S(2)}) collective-permute-start(f32[1,16,4096]{2,1,0:T(8,128)S(1)} %add_select_fusion.3), channel_id=1, source_target_pairs={{0,16},{16,0},{2,18},{18,2},{4,20},{20,4},{6,22},{22,6},{8,24},{24... | collective-permute-start | bytes 786440 | tf_op jit(solution)/shard_map/ppermute | solution.py:23
  62.3 0.2 convolution_bitcast_fusion.2
  62.6 6.8 %collective-permute-done.8 = f32[1,16,4096]{2,1,0:T(8,128)S(1)} collective-permute-done((f32[1,16,4096]{2,1,0:T(8,128)S(1)}, f32[1,16,4096]{2,1,0:T(8,128)S(1)}, u32[]{:S(2)}, u32[]{:S(2)}) %collective-permute-start.8) | collective-permute-done | bytes 262176 | tf_op jit(solution)/shard_map/ppermute | solution.py:23
  69.6 0.2 reshape.310
  69.8 0.6 fusion.1
  70.5 1.3 %fusion = f32[128,1,16,64]{0,3,2,1:T(8,128)S(1)} fusion(f32[128,1,16,64]{0,3,2,1:T(8,128)S(1)} %fusion.1, bf16[128,16,64]{0,2,1:T(8,128)(2,1)S(1)} %bitcast.113, f32[128,16]{0,1:T(8,128)S(1)} %compare_select_fusion, f32[128,128]{1,0:T(8,128)S(1)} %copy.24, f32[128,16]{0,1:T(8,128)S(1)} %bitcast.118, pred[128,128]{1,0:T(8,128)(4,1)S(1)} %iota_compare_fusion), kind=kOutput, calls=%fused_computation.2 | convolution fusion | flops 202506240 | bytes 1409024 | tf_op jit(solution)/shard_map/tsch,schp->tchp/dot_general | solution.py:96
  71.8 0.2 copy.28
  72.0 2.2 %multiply_reduce_fusion = (f32[128]{0:T(128)S(1)}, f32[128,1024]{1,0:T(8,128)S(1)}) fusion(f32[128,1024]{1,0:T(8,128)S(1)} %copy.28, bf16[1024,1024]{1,0:T(8,128)(2,1)} %all-gather.6.cloned.1.call-done, bf16[128,1,1024]{2,0,1:T(8,128)(2,1)S(1)} %copy-done), kind=kOutput, calls=%fused_computation.28 | convolution fusion | flops 269614976 | bytes 3408384 | tf_op jit(solution)/shard_map/dot_general | solution.py:74
  74.2 2.8 %fusion.3 = bf16[128,1,1024]{2,0,1:T(8,128)(2,1)} fusion(bf16[1024,1024]{1,0:T(8,128)(2,1)} %all-gather.8.cloned.1.call-done, f32[128,1024]{1,0:T(8,128)S(1)} %get-tuple-element.28, f32[1024]{0:T(1024)S(1)} %copy-done.2, f32[128]{0:T(128)S(1)} %add_rsqrt_fusion), kind=kOutput, calls=%fused_computation.8 | convolution fusion | flops 268959744 | bytes 2888192 | tf_op jit(solution)/shard_map/dot_general | solution.py:133
  (49 shorter events, 1.8 us)
Async XLA Ops:
  6.5 6.0 %copy-start = (bf16[128,1,1024]{2,0,1:T(8,128)(2,1)S(1)}, bf16[128,1,1024]{2,0,1:T(8,128)(2,1)}, u32[]{:S(2)}) copy-start(bf16[128,1,1024]{2,0,1:T(8,128)(2,1)} %param.11) | copy-start | bytes 786436
  6.5 14.7 %copy-start.3 = (f32[4,128]{1,0:T(4,128)S(1)}, f32[4,128]{1,0:T(4,128)}, u32[]{:S(2)}) copy-start(f32[4,128]{1,0:T(4,128)} %param.17) | copy-start | bytes 6148
  6.5 14.8 %copy-start.1 = (f32[4,1024]{1,0:T(4,128)S(1)}, f32[4,1024]{1,0:T(4,128)}, u32[]{:S(2)}) copy-start(f32[4,1024]{1,0:T(4,128)} %param.16) | copy-start | bytes 49156
  6.5 17.1 %all-gather.4.cloned.1.call-start = ((), (), s32[]{:S(2)}) async-start(), calls=%async_computation.1 | async-start | bytes 3145728 | tf_op jit(solution)/shard_map/all_gather | solution.py:62
  7.3 64.7 %all-gather.6.cloned.1.call-start = ((), (), s32[]{:S(2)}) async-start(), calls=%async_computation.2 | async-start | bytes 3145728 | tf_op jit(solution)/shard_map/all_gather | solution.py:63
  13.7 7.7 %collective-permute-start.2 = (f32[1,16]{1,0:T(1,128)S(1)}, f32[1,16]{1,0:T(1,128)S(1)}, u32[]{:S(2)}, u32[]{:S(2)}) collective-permute-start(f32[1,16]{1,0:T(1,128)S(1)} %get-tuple-element.11), channel_id=1, source_target_pairs={{0,2},{2,0},{4,6},{6,4},{8,10},{10,8},{12,14},{14,12},{16,18},{18,... | collective-permute-start | bytes 200 | tf_op jit(solution)/shard_map/ppermute | solution.py:23
  19.2 4.4 %collective-permute-start.1 = (bf16[3,1,128]{2,0,1:T(4,128)(2,1)S(1)}, bf16[3,1,128]{2,0,1:T(4,128)(2,1)S(1)}, u32[]{:S(2)}, u32[]{:S(2)}) collective-permute-start(bf16[3,1,128]{2,0,1:T(4,128)(2,1)S(1)} %slice_bitcast_fusion.3), channel_id=1, source_target_pairs={{0,2},{2,4},{4,6},{6,8},{8,10},{10,12},{12,14},{14,16},{16,18},{18... | collective-permute-start | bytes 2312 | tf_op jit(solution)/shard_map/ppermute | solution.py:13
  21.1 53.1 %all-gather.8.cloned.1.call-start = ((), (), s32[]{:S(2)}) async-start(), calls=%async_computation.3 | async-start | bytes 3145728 | tf_op jit(solution)/shard_map/all_gather | solution.py:135
  21.4 13.9 %collective-permute-start.3 = (f32[1,16]{1,0:T(1,128)S(1)}, f32[1,16]{1,0:T(1,128)S(1)}, u32[]{:S(2)}, u32[]{:S(2)}) collective-permute-start(f32[1,16]{1,0:T(1,128)S(1)} %get-tuple-element.10), channel_id=1, source_target_pairs={{0,4},{4,0},{2,6},{6,2},{8,12},{12,8},{10,14},{14,10},{16,20},{20,... | collective-permute-start | bytes 200 | tf_op jit(solution)/shard_map/ppermute | solution.py:23
  25.7 5.7 %collective-permute-start = (bf16[3,1,1024]{2,0,1:T(4,128)(2,1)S(1)}, bf16[3,1,1024]{2,0,1:T(4,128)(2,1)S(1)}, u32[]{:S(2)}, u32[]{:S(2)}) collective-permute-start(bf16[3,1,1024]{2,0,1:T(4,128)(2,1)S(1)} %slice_bitcast_fusion.2), channel_id=1, source_target_pairs={{0,2},{2,4},{4,6},{6,8},{8,10},{10,12},{12,14},{14,16},{16,18},{18... | collective-permute-start | bytes 18440 | tf_op jit(solution)/shard_map/ppermute | solution.py:13
  32.7 7.8 %collective-permute-start.5 = (f32[1,16,4096]{2,1,0:T(8,128)S(1)}, f32[1,16,4096]{2,1,0:T(8,128)S(1)}, u32[]{:S(2)}, u32[]{:S(2)}) collective-permute-start(f32[1,16,4096]{2,1,0:T(8,128)S(1)} %reshape.309), channel_id=1, source_target_pairs={{0,2},{2,0},{4,6},{6,4},{8,10},{10,8},{12,14},{14,12},{16,18},{18,... | collective-permute-start | bytes 786440 | tf_op jit(solution)/shard_map/ppermute | solution.py:23
  35.3 5.2 %collective-permute-start.4 = (f32[1,16]{1,0:T(1,128)S(1)}, f32[1,16]{1,0:T(1,128)S(1)}, u32[]{:S(2)}, u32[]{:S(2)}) collective-permute-start(f32[1,16]{1,0:T(1,128)S(1)} %get-tuple-element.8), channel_id=1, source_target_pairs={{0,8},{8,0},{2,10},{10,2},{4,12},{12,4},{6,14},{14,6},{16,24},{24,... | collective-permute-start | bytes 200 | tf_op jit(solution)/shard_map/ppermute | solution.py:23
  40.7 7.3 %collective-permute-start.6 = (f32[1,16,4096]{2,1,0:T(8,128)S(1)}, f32[1,16,4096]{2,1,0:T(8,128)S(1)}, u32[]{:S(2)}, u32[]{:S(2)}) collective-permute-start(f32[1,16,4096]{2,1,0:T(8,128)S(1)} %add_select_fusion.5), channel_id=1, source_target_pairs={{0,4},{4,0},{2,6},{6,2},{8,12},{12,8},{10,14},{14,10},{16,20},{20,... | collective-permute-start | bytes 786440 | tf_op jit(solution)/shard_map/ppermute | solution.py:23
  48.1 10.7 %collective-permute-start.7 = (f32[1,16,4096]{2,1,0:T(8,128)S(1)}, f32[1,16,4096]{2,1,0:T(8,128)S(1)}, u32[]{:S(2)}, u32[]{:S(2)}) collective-permute-start(f32[1,16,4096]{2,1,0:T(8,128)S(1)} %add_select_fusion.4), channel_id=1, source_target_pairs={{0,8},{8,0},{2,10},{10,2},{4,12},{12,4},{6,14},{14,6},{16,24},{24,... | collective-permute-start | bytes 786440 | tf_op jit(solution)/shard_map/ppermute | solution.py:23
  58.9 10.6 %collective-permute-start.8 = (f32[1,16,4096]{2,1,0:T(8,128)S(1)}, f32[1,16,4096]{2,1,0:T(8,128)S(1)}, u32[]{:S(2)}, u32[]{:S(2)}) collective-permute-start(f32[1,16,4096]{2,1,0:T(8,128)S(1)} %add_select_fusion.3), channel_id=1, source_target_pairs={{0,16},{16,0},{2,18},{18,2},{4,20},{20,4},{6,22},{22,6},{8,24},{24... | collective-permute-start | bytes 786440 | tf_op jit(solution)/shard_map/ppermute | solution.py:23
  72.0 2.3 %copy-start.2 = (f32[1024]{0:T(1024)S(1)}, f32[1024]{0:T(1024)}, u32[]{:S(2)}) copy-start(f32[1024]{0:T(1024)} %param.20) | copy-start | bytes 12292
Sparse Core Ops, SparseCore 0:
  8.9 13.2 all-gather.3
  23.8 11.7 all-gather.5
  52.2 8.9 all-gather.7
